TPU v7x, 32 devices: a whole 2x2x4 slice. The times are simulated.
32 devices in a mesh: cfg: 2 (over core), tp: 8 (over z, x), dp: 2 (over y).
Axes of the slice: x: 2, y: 2, z: 4, core: 2. Of those that a mesh axis runs over, the one named last changes fastest.
Arguments:
- tokens: bfloat16 [4096, 512], P('dp'), parts along dimension 0, may hold values from -6 to 6
- conditions: float32 [4, 256], P(('dp', 'cfg')), parts along dimension 0, may hold values from -6 to 6
- ada_block: bfloat16 [256, 3072], P(None, 'tp'), may hold values from -1 to 1
- ada_final: bfloat16 [256, 1024], P(None, 'tp'), may hold values from -1 to 1
- qkv_weight: bfloat16 [512, 3, 512], P(None, None, 'tp'), may hold values from -0.25 to 0.25
- out_weight: bfloat16 [512, 512], P('tp'), may hold values from -0.25 to 0.25
- up_weight: bfloat16 [512, 2048], P(None, 'tp'), may hold values from -0.25 to 0.25
- down_weight: bfloat16 [2048, 512], P('tp'), may hold values from -0.125 to 0.125
- final_weight: bfloat16 [512, 64], replicated, may hold values from -0.25 to 0.25
Outputs:
- guided: float32 [4096, 64], P('dp'), parts along dimension 0
There are 2 independent parts, one for each index of `dp`. A program takes and returns all parts, laid end to end along the dimension named above; an argument that names none is the same for every part. Nothing has to cross between parts.
All inputs are finite; a program needn't handle non-finite values.
Results may differ from a plain program's by a relative error of at most 0.02.
Values may be sent and summed in bfloat16 or wider, within the bound.
A program may use at most 128 MiB of HBM per device.

v0:
```python
import jax
import jax.numpy as jnp
from jax import lax
from jax.sharding import PartitionSpec as P

HEAD_SIZE = 64


guidance = 4.0
epsilon = 1e-06


def layer_norm(values):
    average = jnp.mean(values, -1, keepdims=True)
    centred = values - average
    spread = jnp.mean(centred * centred, -1, keepdims=True)
    return centred * lax.rsqrt(spread + epsilon)


def modulate(stream, scales, shifts):
    return (layer_norm(stream) * (1.0 + scales) + shifts).astype(jnp.bfloat16)


def attend(projected):
    token_count = projected.shape[0]
    local_width = projected.shape[2]
    local_heads = local_width // HEAD_SIZE
    per_head = projected.reshape(token_count, 3, local_heads, HEAD_SIZE)
    scores = jnp.einsum(
        "thd,shd->hts", per_head[:, 0], per_head[:, 1], preferred_element_type=jnp.float32
    ) * HEAD_SIZE ** (-0.5)
    softmaxed = jax.nn.softmax(scores, axis=-1)
    values_f = per_head[:, 2].astype(jnp.float32)
    head_out = jnp.einsum("hts,shd->thd", softmaxed, values_f)
    return head_out.reshape(token_count, local_width).astype(jnp.bfloat16)


def local(
    tokens,
    conditions,
    ada_block,
    ada_final,
    qkv_weight,
    out_weight,
    up_weight,
    down_weight,
    final_weight,
):
    model_width = tokens.shape[1]
    signal = jax.nn.silu(conditions).astype(jnp.bfloat16)
    block_local = jnp.dot(signal, ada_block, preferred_element_type=jnp.float32)[0]
    final_local = jnp.dot(signal, ada_final, preferred_element_type=jnp.float32)[0]
    shifts, final_mod = (
        lax.all_gather(block_local, "tp", axis=0, tiled=True),
        lax.all_gather(final_local, "tp", axis=0, tiled=True),
    )
    shifts = shifts.reshape(6, model_width)
    stream = tokens.astype(jnp.float32)
    normed = modulate(stream, shifts[1], shifts[0])
    projected = jnp.einsum(
        "td,dke->tke", normed, qkv_weight, preferred_element_type=jnp.float32
    ).astype(jnp.bfloat16)
    head_out = attend(projected)
    attended = lax.psum(
        jnp.dot(head_out, out_weight, preferred_element_type=jnp.float32).astype(jnp.bfloat16), "tp"
    ).astype(jnp.float32)
    stream = stream + shifts[2] * attended
    normed = modulate(stream, shifts[4], shifts[3])
    upward = jnp.dot(normed, up_weight, preferred_element_type=jnp.float32)
    hidden = jax.nn.gelu(upward, approximate=True).astype(jnp.bfloat16)
    mlp_out = lax.psum(
        jnp.dot(hidden, down_weight, preferred_element_type=jnp.float32).astype(jnp.bfloat16), "tp"
    ).astype(jnp.float32)
    stream = stream + shifts[5] * mlp_out
    final_mod = final_mod.reshape(2, model_width)
    final_in = modulate(stream, final_mod[1], final_mod[0])
    predicted = jnp.dot(final_in, final_weight, preferred_element_type=jnp.float32)
    is_cond = lax.axis_index("cfg") == 0
    weighting = jnp.where(is_cond, guidance, 1.0 - guidance).astype(jnp.float32)
    return lax.psum((weighting * predicted).astype(jnp.bfloat16), "cfg").astype(jnp.float32)


def solution(mesh):
    placed = (
        P("dp", None),
        P(("dp", "cfg"), None),
        P(None, "tp"),
        P(None, "tp"),
        P(None, None, "tp"),
        P("tp", None),
        P(None, "tp"),
        P("tp", None),
        P(),
    )
    return jax.shard_map(
        local, mesh=mesh, in_specs=placed, out_specs=P("dp", None), check_vma=False
    )
```

profile of v0, /device:TPU:0, one launch (start us, length us, event | category | flops | bytes accessed | tf_op | source)
XLA Modules:
  0.0 319.5 jit_solution(2466030839063625285)
XLA Ops:
  6.5 0.0 copy-start
  6.5 0.0 copy-start.1
  6.5 0.0 copy-start.8
  6.5 0.0 all-reduce.4.cloned.1.call-start
  6.5 1.2 convolution_bitcast_fusion
  7.8 32.3 %all-gather = f32[8,1,384]{2,1,0:T(1,128)S(1)} all-gather(f32[1,1,384]{2,1,0:T(1,128)S(1)} %convolution_bitcast_fusion), channel_id=1, replica_groups=mesh['cfg'=2,'tp'=8,'dp'=2] {'tp'}, dimensions={0}, use_global_device_ids=true | all-gather | bytes 13824 | tf_op jit(solution)/shard_map/all_gather | solution.py:54
  40.1 1.9 convert_reduce_fusion
  42.0 2.5 fusion.8
  44.5 0.0 copy-done.1
  44.5 0.0 copy-done.8
  44.5 1.2 fusion.28
  45.8 0.1 convert_bitcast_fusion
  45.9 8.1 %multiply_reduce_fusion = (f32[2048]{0:T(1024)S(1)}, f32[2048,2048]{0,1:T(8,128)}) fusion(bf16[2048,3,1,64]{0,3,1,2:T(8,128)(2,1)S(1)} %convert_bitcast_fusion), kind=kOutput, calls=%fused_computation.3 | convolution fusion | flops 545257472 | bytes 17309696 | tf_op jit(solution)/shard_map/thd,shd->hts/dot_general | solution.py:29
  53.9 0.0 copy-start.9
  53.9 8.6 %fusion.2 = f32[2048]{0:T(1024)S(1)} fusion(f32[2048,2048]{0,1:T(8,128)} %get-tuple-element.14, f32[2048]{0:T(1024)S(1)} %get-tuple-element.13), kind=kLoop, calls=%fused_computation.4 | loop fusion | flops 12580864 | bytes 16793600 | tf_op jit(solution)/shard_map/reduce_sum | solution.py:32
  62.5 0.0 copy-done.9
  62.5 8.9 %convolution_convert_fusion.1 = bf16[2048,512]{1,0:T(8,128)(2,1)} fusion(bf16[64,512]{1,0:T(8,128)(2,1)S(1)} %copy-done.9, f32[2048,2048]{0,1:T(8,128)} %get-tuple-element.14, f32[2048]{0:T(1024)S(1)} %fusion.2, f32[2048]{0:T(1024)S(1)} %get-tuple-element.13, bf16[2048,3,1,64]{0,3,1,2:T(8,128)(2,1)S(1)} %convert_bitcast_fusion), kind=kOutput, calls=%fused_computation.24 | convolution fusion | flops 684851200 | bytes 19218432 | tf_op jit(solution)/shard_map/dot_general | solution.py:65
  71.5 0.0 all-reduce.4.cloned.1.call-update
  71.5 0.2 all-reduce.6.cloned.1.call-start
  71.7 103.2 %all-reduce.4.cloned.1.call-done = bf16[2048,512]{1,0:T(8,128)(2,1)} async-done(((bf16[2048,512]{1,0:T(8,128)(2,1)}), bf16[2048,512]{1,0:T(8,128)(2,1)}) %all-reduce.4.cloned.1.call-update) | async-done | bytes 2097168 | tf_op jit(solution)/shard_map/psum | solution.py:64
  174.9 0.0 copy-start.2
  174.9 0.0 copy-start.7
  174.9 2.5 fusion.12
  177.4 0.0 copy-done.2
  177.4 1.2 multiply_reduce_fusion.2
  178.6 0.0 copy-done
  178.6 0.0 copy-done.7
  178.6 0.0 copy-start.5
  178.6 0.0 copy-start.6
  178.6 5.1 %convolution_convert_fusion = bf16[2048,512]{1,0:T(8,128)(2,1)} fusion(bf16[256,512]{1,0:T(8,128)(2,1)S(1)} %copy-done, bf16[512,256]{1,0:T(8,128)(2,1)S(1)} %copy-done.7, bf16[2048,512]{1,0:T(8,128)(2,1)} %all-reduce.4.cloned.1.call-done, bf16[2048,512]{1,0:T(8,128)(2,1)S(1)} %copy-done.1, f32[512]{0:T(512)S(1)} %get-tuple-element.6, ...), kind=kOutput, calls=%fused_computation.23 | convolution fusion | flops 1088946176 | bytes 6838272 | tf_op jit(solution)/shard_map/dot_general | solution.py:72
  183.7 0.0 all-reduce.6.cloned.1.call-update
  183.8 0.0 all-reduce.8.cloned.1.call-start
  183.8 0.0 copy-done.5
  183.8 0.0 copy-done.6
  183.8 0.1 convolution_bitcast_fusion.1
  184.0 19.0 %all-gather.1 = f32[8,1,128]{2,1,0:T(1,128)S(1)} all-gather(f32[1,1,128]{2,1,0:T(1,128)S(1)} %convolution_bitcast_fusion.1), channel_id=1, replica_groups=mesh['cfg'=2,'tp'=8,'dp'=2] {'tp'}, dimensions={0}, use_global_device_ids=true | all-gather | bytes 4608 | tf_op jit(solution)/shard_map/all_gather | solution.py:55
  203.0 82.7 %all-reduce.6.cloned.1.call-done = bf16[2048,512]{1,0:T(8,128)(2,1)} async-done(((bf16[2048,512]{1,0:T(8,128)(2,1)}), bf16[2048,512]{1,0:T(8,128)(2,1)}) %all-reduce.6.cloned.1.call-update) | async-done | bytes 2097168 | tf_op jit(solution)/shard_map/psum | solution.py:71
  285.6 0.0 copy-start.3
  285.6 0.0 copy-start.4
  285.6 3.5 %fusion.45 = f32[2048]{0:T(1024)S(1)} fusion(bf16[2048,512]{1,0:T(8,128)(2,1)} %all-reduce.6.cloned.1.call-done, f32[512]{0:T(512)S(1)} %get-tuple-element.5, bf16[2048,512]{1,0:T(8,128)(2,1)} %all-reduce.4.cloned.1.call-done, f32[512]{0:T(512)S(1)} %get-tuple-element.10, bf16[2048,512]{1,0:T(8,128)(2,1)S(1)} %copy-done.1), kind=kLoop, calls=%fused_computation.58 | loop fusion | flops 8386560 | bytes 6303744 | tf_op jit(solution)/shard_map/reduce_sum | solution.py:14
  289.2 0.0 copy-start.10
  289.2 0.0 copy-done.3
  289.2 0.0 copy-done.4
  289.2 1.6 multiply_reduce_fusion.1
  290.8 0.0 copy-done.10
  290.8 2.7 fusion.13
  293.5 0.0 all-reduce.8.cloned.1.call-update
  293.5 17.7 %all-reduce.8.cloned.1.call-done = bf16[2048,64]{0,1:T(8,128)(2,1)} async-done(((bf16[2048,64]{0,1:T(8,128)(2,1)}), bf16[2048,64]{0,1:T(8,128)(2,1)}) %all-reduce.8.cloned.1.call-update) | async-done | bytes 262160 | tf_op jit(solution)/shard_map/psum | solution.py:80
  311.2 1.8 convert_element_type.68
  (8 shorter events, 0.0 us)
Async XLA Ops:
  6.5 172.0 %copy-start = (bf16[256,512]{1,0:T(8,128)(2,1)S(1)}, bf16[256,512]{1,0:T(8,128)(2,1)}, u32[]{:S(2)}) copy-start(bf16[256,512]{1,0:T(8,128)(2,1)} %param.16) | copy-start | bytes 786436
  6.5 38.0 %copy-start.1 = (bf16[2048,512]{1,0:T(8,128)(2,1)S(1)}, bf16[2048,512]{1,0:T(8,128)(2,1)}, u32[]{:S(2)}) copy-start(bf16[2048,512]{1,0:T(8,128)(2,1)} %param.9) | copy-start | bytes 6291460
  6.5 38.0 %copy-start.8 = (bf16[512,3,64]{0,2,1:T(8,128)(2,1)S(1)}, bf16[512,3,64]{0,2,1:T(8,128)(2,1)}, u32[]{:S(2)}) copy-start(bf16[512,3,64]{0,2,1:T(8,128)(2,1)} %param.13) | copy-start | bytes 589828
  6.5 168.3 %all-reduce.4.cloned.1.call-start = ((), (), s32[]{:S(2)}) async-start(), calls=%async_computation | async-start | bytes 4194304 | tf_op jit(solution)/shard_map/psum | solution.py:64
  53.9 8.6 %copy-start.9 = (bf16[64,512]{1,0:T(8,128)(2,1)S(1)}, bf16[64,512]{1,0:T(8,128)(2,1)}, u32[]{:S(2)}) copy-start(bf16[64,512]{1,0:T(8,128)(2,1)} %param.14) | copy-start | bytes 196612
  71.5 214.2 %all-reduce.6.cloned.1.call-start = ((), (), s32[]{:S(2)}) async-start(), calls=%async_computation.1 | async-start | bytes 4194304 | tf_op jit(solution)/shard_map/psum | solution.py:71
  174.9 2.5 copy-start.2
  174.9 3.7 %copy-start.7 = (bf16[512,256]{1,0:T(8,128)(2,1)S(1)}, bf16[512,256]{1,0:T(8,128)(2,1)}, u32[]{:S(2)}) copy-start(bf16[512,256]{1,0:T(8,128)(2,1)} %param.15) | copy-start | bytes 786436
  178.6 5.2 %copy-start.5 = (bf16[256,128]{1,0:T(8,128)(2,1)S(1)}, bf16[256,128]{1,0:T(8,128)(2,1)}, u32[]{:S(2)}) copy-start(bf16[256,128]{1,0:T(8,128)(2,1)} %param.12) | copy-start | bytes 196612
  178.6 5.2 %copy-start.6 = (f32[1,256]{1,0:T(1,128)S(1)}, f32[1,256]{1,0:T(1,128)}, u32[]{:S(2)}) copy-start(f32[1,256]{1,0:T(1,128)} %param.10) | copy-start | bytes 3076
  183.8 127.5 %all-reduce.8.cloned.1.call-start = ((), (), s32[]{:S(2)}) async-start(), calls=%async_computation.2 | async-start | bytes 524288 | tf_op jit(solution)/shard_map/psum | solution.py:80
  285.6 3.6 %copy-start.3 = (bf16[2048,512]{1,0:T(8,128)(2,1)S(1)}, bf16[2048,512]{1,0:T(8,128)(2,1)}, u32[]{:S(2)}) copy-start(bf16[2048,512]{1,0:T(8,128)(2,1)} %all-reduce.4.cloned.1.call-done) | copy-start | bytes 6291460
  285.6 3.6 %copy-start.4 = (bf16[2048,512]{1,0:T(8,128)(2,1)S(1)}, bf16[2048,512]{1,0:T(8,128)(2,1)}, u32[]{:S(2)}) copy-start(bf16[2048,512]{1,0:T(8,128)(2,1)} %all-reduce.6.cloned.1.call-done) | copy-start | bytes 6291460
  289.2 1.7 copy-start.10
Sparse Core Ops, SparseCore 0:
  71.6 103.2 all-reduce.3
  183.9 101.7 all-reduce.5
  293.7 17.5 all-reduce.7
where the time goes:
time: 320 us
  waiting for transfers between devices  204 us (64%)
  blocking collectives  51.3 us (16%)
  matrix products  27.3 us (9%)
  other arithmetic  23.7 us (7%)
  between operations  13.3 us (4%)
    psum x1, waiting for transfers between devices, local(): lax.psum(jnp.dot(head_out, out_weight, preferred_element_type=jnp.float32...  103 us
    psum x1, waiting for transfers between devices, local(): lax.psum(jnp.dot(hidden, down_weight, preferred_element_type=jnp.float32)...  82.7 us
    all_gather x1, blocking collectives, local(): lax.all_gather(block_local, 'tp', axis=0, tiled=True)  32.3 us
    all_gather x1, blocking collectives, local(): lax.all_gather(final_local, 'tp', axis=0, tiled=True)  19 us
    psum x1, waiting for transfers between devices, local(): lax.psum((weighting * predicted).astype(jnp.bfloat16), 'cfg')  17.7 us
    dot_general x1, matrix products, local(): jnp.dot(head_out, out_weight, preferred_element_type=jnp.float32)  8.92 us
    reduce_sum x1, other arithmetic, attend(): softmaxed = jax.nn.softmax(scores, axis=-1)  8.58 us
    dot_general x1, matrix products, attend(): jnp.einsum('thd,shd->hts', per_head[:, 0], per_head[:, 1], preferred_elem...  8.09 us
  transfers between devices with their start and end apart: 3, of which 3 were waited for; matrix products, arithmetic and copies ran while one was open for 0% of the time, Pallas kernels for 0%

commit v1 on v0

--- a/solution.py
+++ b/solution.py
@@ -1,10 +1,16 @@
+import functools
+import math
+
 import jax
 import jax.numpy as jnp
 from jax import lax
+from jax.experimental import pallas as pl
+from jax.experimental.pallas import tpu as pltpu
 from jax.sharding import PartitionSpec as P
 
 HEAD_SIZE = 64
-
+MESH = pl.DeviceIdType.MESH
+F32, BF16 = jnp.float32, jnp.bfloat16
 
 guidance = 4.0
 epsilon = 1e-06
@@ -18,7 +24,338 @@
 
 
 def modulate(stream, scales, shifts):
-    return (layer_norm(stream) * (1.0 + scales) + shifts).astype(jnp.bfloat16)
+    return (layer_norm(stream) * (1.0 + scales) + shifts).astype(BF16)
+
+
+def dot(a, b):
+    return jnp.dot(a, b, preferred_element_type=F32)
+
+
+def dot_nt(a, b):
+    return lax.dot_general(a, b, (((1,), (1,)), ((), ())), preferred_element_type=F32)
+
+
+def remote(src, dst, send, recv, where):
+    return pltpu.make_async_remote_copy(
+        src_ref=src, dst_ref=dst, send_sem=send, recv_sem=recv, device_id=where, device_id_type=MESH
+    )
+
+
+def rows_of(ref, start, count):
+    return ref.at[pl.ds(pl.multiple_of(start, count), count)]
+
+
+def block_kernel(
+    n,
+    tokens, cond, ada_block, ada_final, qkv, out_w, up_w, down_w, final_w,
+    result,
+    mod_mine, mod_all, xhat, q_s, k_s, v_s, ho_mine, ho_all, f_out, f_up, f_down,
+    half_out, half_in, fin_buf,
+    mod_send, mod_recv, ho_send, ho_recv, g_send, g_recv, h_sem, p_send, p_recv, d_send, d_recv,
+):
+    me = lax.axis_index("tp")
+    c = lax.axis_index("cfg")
+    other = {"cfg": 1 - c}
+    count, width = tokens.shape
+    shard = count // n
+    nz = n // 2
+    x, z = lax.rem(me, 2), me // 2
+
+    def at(col, dz):
+        return lax.rem(z + dz + nz, nz) * 2 + lax.rem(x + col, 2)
+
+    barrier = pltpu.get_barrier_semaphore()
+    for d in range(1, n):
+        pl.semaphore_signal(
+            barrier, inc=1, device_id={"tp": lax.rem(me + d, n)}, device_id_type=MESH
+        )
+    pl.semaphore_signal(barrier, inc=1, device_id=other, device_id_type=MESH)
+
+    raw = cond[...]
+    signal = jnp.broadcast_to(raw / (1.0 + jnp.exp(-raw)), (8, raw.shape[1])).astype(BF16)
+    nb, nf = ada_block.shape[1], ada_final.shape[1]
+    mod_mine[0, :, :nb] = dot(signal, ada_block[...])[0:1]
+    mod_mine[0, :, nb:] = dot(signal, ada_final[...])[0:1]
+    pl.semaphore_wait(barrier, n)
+
+    def mod_copy(d):
+        return remote(
+            mod_mine.at[0], mod_all.at[me], mod_send.at[d - 1], mod_recv.at[d - 1],
+            {"tp": lax.rem(me + d, n)},
+        )
+
+    for d in range(1, n):
+        mod_copy(d).start()
+
+    own = (out_w, up_w, down_w)
+    full = (f_out, f_up, f_down)
+    places = [
+        (at(1, 0), 0), (at(0, -1), 0), (at(0, 1), 0), (at(1, -1), 0), (at(1, 1), 0),
+        (at(0, 2), 1), (at(0, 2), 2), (at(1, 2), 1), (at(1, 2), 2),
+    ]
+
+    def region(ref, part, core):
+        rows = ref.shape[0]
+        if part == 0:
+            return rows_of(ref, core * (rows // 2), rows // 2)
+        return rows_of(ref, core * (rows // 2) + (part - 1) * (rows // 4), rows // 4)
+
+    plus, minus, across = {"tp": at(0, 1)}, {"tp": at(0, -1)}, {"tp": at(1, 0)}
+    sends = [
+        (me, 0, across), (me, 0, plus), (me, 0, minus),
+        (at(1, 0), 0, plus), (at(1, 0), 0, minus),
+        (at(0, -1), 1, plus), (at(0, 1), 2, minus),
+        (at(1, -1), 1, plus), (at(1, 1), 2, minus),
+    ]
+    links = len(sends)
+
+    def link(k, j):
+        owner, part, where = sends[j]
+        src = own[k] if j < 3 else full[k].at[owner]
+        return remote(
+            region(src, part, c), region(full[k].at[owner], part, c),
+            g_send.at[k, j], g_recv.at[k, j], where,
+        )
+
+    def landed(k, j):
+        owner, part = places[j]
+        dst = region(full[k].at[owner], part, c)
+        return remote(dst, dst, g_send.at[k, j], g_recv.at[k, j], across)
+
+    def share(k, j):
+        owner, part = places[j]
+        dst = region(full[k].at[owner], part, c)
+        return remote(dst, dst, g_send.at[k, links + j], g_recv.at[k, links + j], other)
+
+    def shared(k, j):
+        owner, part = places[j]
+        dst = region(full[k].at[owner], part, 1 - c)
+        return remote(dst, dst, g_send.at[k, links + j], g_recv.at[k, links + j], other)
+
+    def open_gather(k):
+        for j in (0, 1, 2):
+            link(k, j).start()
+
+    def forward(k, arrivals, starts):
+        for j in arrivals:
+            landed(k, j).wait_recv()
+        for j in starts:
+            link(k, j).start()
+        for j in arrivals:
+            share(k, j).start()
+
+    open_gather(0)
+    open_gather(1)
+    for k in range(3):
+        full[k][me] = own[k][...]
+
+    def norm_step(i, _):
+        r = pl.ds(pl.multiple_of(i * shard, shard), shard)
+        xhat[r, :] = layer_norm(tokens[r, :].astype(F32))
+        return 0
+
+    lax.fori_loop(0, count // shard, norm_step, 0)
+
+    mod_all[me] = mod_mine[0]
+    for d in range(1, n):
+        origin = mod_all.at[lax.rem(me - d + n, n)]
+        remote(origin, origin, mod_send.at[d - 1], mod_recv.at[d - 1], across).wait_recv()
+
+    def mod_row(base, per, row):
+        lane = math.gcd(per, width)
+        pieces = []
+        for g in range(row * width // lane, (row + 1) * width // lane):
+            t, off = (g * lane) // per, (g * lane) % per
+            pieces.append(mod_all[t, :, base + off : base + off + lane])
+        return jnp.concatenate(pieces, axis=1)
+
+    shift1, scale1, gate1, shift2, scale2, gate2 = [mod_row(0, nb, r) for r in range(6)]
+    shift_f, scale_f = [mod_row(nb, nf, r) for r in range(2)]
+
+    h = HEAD_SIZE
+    ones = (lax.broadcasted_iota(jnp.int32, (shard, h), 1) == 0).astype(F32).astype(BF16)
+
+    def qkv_step(i, _):
+        r = pl.ds(pl.multiple_of(i * shard, shard), shard)
+        normed = (xhat[r, :] * (1.0 + scale1) + shift1).astype(BF16)
+        q_s[r, :] = (dot(normed, qkv[0]) * (h ** -0.5 * math.log2(math.e))).astype(BF16)
+        k_s[r, :] = dot(normed, qkv[1]).astype(BF16)
+        v_s[r, :h] = dot(normed, qkv[2]).astype(BF16)
+        v_s[r, h:] = ones
+        return 0
+
+    lax.fori_loop(0, count // shard, qkv_step, 0)
+
+    def ho_copy(i):
+        return remote(
+            ho_mine.at[i], ho_all.at[me], ho_send.at[i], ho_recv.at[i],
+            {"tp": lax.rem(me + 1 + i, n)},
+        )
+
+    sub = shard // 2
+
+    def attend_step(i, _):
+        @pl.when(i == 0)
+        def _():
+            for k in (0, 1):
+                forward(k, (0, 1, 2), (3, 4, 5, 6))
+            open_gather(2)
+
+        @pl.when(i == 3)
+        def _():
+            for k in (0, 1):
+                forward(k, (3, 4), (7, 8))
+
+        @pl.when(i == 4)
+        def _():
+            forward(2, (0, 1, 2), (3, 4, 5, 6))
+            for k in (0, 1):
+                forward(k, (5, 6), ())
+
+        @pl.when(i == 6)
+        def _():
+            forward(2, (3, 4), (7, 8))
+            for k in (0, 1):
+                forward(k, (7, 8), ())
+
+        peer = lax.rem(me + 1 + i, n)
+        for part in range(shard // sub):
+            r = pl.ds(pl.multiple_of(peer * shard + part * sub, sub), sub)
+            scores = dot_nt(q_s[r, :], k_s[...])
+            top = jnp.max(scores, axis=-1, keepdims=True)
+            weights = jnp.exp2(scores - top).astype(BF16)
+            mixed = dot(weights, v_s[...])
+            ho_mine[i, part * sub : (part + 1) * sub, :] = (
+                mixed[:, :h] / mixed[:, h : h + 1]
+            ).astype(BF16)
+
+        @pl.when(i < n - 1)
+        def _():
+            ho_copy(i).start()
+
+        return 0
+
+    lax.fori_loop(0, n, attend_step, 0)
+    forward(2, (5, 6), ())
+
+    ho_all[me] = ho_mine[n - 1]
+    for j in range(links):
+        shared(0, j).wait_recv()
+    for i in range(n - 1):
+        origin = ho_all.at[lax.rem(me - 1 - i + n, n)]
+        remote(origin, origin, ho_send.at[i], ho_recv.at[i], across).wait_recv()
+    attended = dot(ho_all[0], f_out[0])
+    for t in range(1, n):
+        attended += dot(ho_all[t], f_out[t])
+    r = pl.ds(pl.multiple_of(me * shard, shard), shard)
+    stream = tokens[r, :].astype(F32) + gate1 * attended
+    normed = modulate(stream, scale2, shift2)
+    forward(2, (7, 8), ())
+    for j in range(links):
+        shared(1, j).wait_recv()
+    hidden = [
+        jax.nn.gelu(dot(normed, f_up[t]), approximate=True).astype(BF16) for t in range(n)
+    ]
+    for j in range(links):
+        shared(2, j).wait_recv()
+    mlp = dot(hidden[0], f_down[0])
+    for t in range(1, n):
+        mlp += dot(hidden[t], f_down[t])
+    stream = stream + gate2 * mlp
+    final_in = modulate(stream, scale_f, shift_f)
+
+    weighting = jnp.where(c == 0, guidance, 1.0 - guidance).astype(F32)
+    out_width = final_w.shape[1]
+    predicted = weighting * dot(final_in, final_w[...])
+    quarter = shard // 4
+    for half in range(2):
+        lo = half * 2 * quarter
+        half_out[half, :, :] = jnp.concatenate(
+            [predicted[lo : lo + quarter], predicted[lo + quarter : lo + 2 * quarter]], axis=1
+        )
+    trade = remote(half_out.at[1 - c], half_in, h_sem.at[0], h_sem.at[1], other)
+    trade.start()
+    trade.wait()
+    fin_buf[me, c] = (half_out[c] + half_in[...]).astype(BF16)
+
+    def push(d):
+        return remote(
+            fin_buf.at[me, c], fin_buf.at[me, c], p_send.at[d], p_recv.at[d],
+            {"tp": lax.rem(me + d, n)},
+        )
+
+    def hand(d, core):
+        place = fin_buf.at[lax.rem(me - d + n, n), core]
+        return remote(place, place, d_send.at[d], d_recv.at[d], other)
+
+    for d in (4, 3, 5, 2, 6, 1, 7):
+        if d < n:
+            push(d).start()
+    hand(0, c).start()
+    for d in range(1, n):
+        place = fin_buf.at[lax.rem(me - d + n, n), c]
+        remote(place, place, p_send.at[d], p_recv.at[d], across).wait_recv()
+        hand(d, c).start()
+    for d in range(n):
+        hand(d, 1 - c).wait_recv()
+    for t in range(n):
+        for half in range(2):
+            both = fin_buf[t, half].astype(F32)
+            lo = t * shard + half * 2 * quarter
+            result[lo : lo + quarter, :] = both[:, :out_width]
+            result[lo + quarter : lo + 2 * quarter, :] = both[:, out_width:]
+
+    for d in range(1, n):
+        mod_copy(d).wait_send()
+        push(d).wait_send()
+        ho_copy(d - 1).wait_send()
+    for d in range(n):
+        hand(d, c).wait_send()
+    for k in range(3):
+        for j in range(links):
+            link(k, j).wait_send()
+            share(k, j).wait_send()
+
+
+def fused(n, tokens, cond, ada_block, ada_final, qkv_weight, out_weight, up_weight, down_weight, final_weight):
+    count, width = tokens.shape
+    shard = count // n
+    qkv = jnp.transpose(qkv_weight, (1, 0, 2))
+    mod = ada_block.shape[1] + ada_final.shape[1]
+    h, out_width = HEAD_SIZE, final_weight.shape[1]
+    dma = pltpu.SemaphoreType.DMA
+    vm = pl.BlockSpec(memory_space=pltpu.VMEM)
+    return pl.pallas_call(
+        functools.partial(block_kernel, n),
+        out_shape=jax.ShapeDtypeStruct((count, out_width), F32),
+        in_specs=[vm] * 9,
+        out_specs=vm,
+        scratch_shapes=[
+            pltpu.VMEM((1, 1, mod), F32),
+            pltpu.VMEM((n, 1, mod), F32),
+            pltpu.VMEM((count, width), F32),
+            pltpu.VMEM((count, h), BF16),
+            pltpu.VMEM((count, h), BF16),
+            pltpu.VMEM((count, 2 * h), BF16),
+            pltpu.VMEM((n, shard, h), BF16),
+            pltpu.VMEM((n, shard, h), BF16),
+            pltpu.VMEM((n,) + out_weight.shape, BF16),
+            pltpu.VMEM((n,) + up_weight.shape, BF16),
+            pltpu.VMEM((n,) + down_weight.shape, BF16),
+            pltpu.VMEM((2, shard // 4, 2 * out_width), F32),
+            pltpu.VMEM((shard // 4, 2 * out_width), F32),
+            pltpu.VMEM((n, 2, shard // 4, 2 * out_width), BF16),
+            dma((n - 1,)), dma((n - 1,)),
+            dma((n - 1,)), dma((n - 1,)),
+            dma((3, 18)), dma((3, 18)),
+            dma((2,)),
+            dma((n,)), dma((n,)),
+            dma((n,)), dma((n,)),
+        ],
+        compiler_params=pltpu.CompilerParams(
+            collective_id=0, has_side_effects=True, vmem_limit_bytes=60 * 1024 * 1024
+        ),
+    )(tokens, cond, ada_block, ada_final, qkv, out_weight, up_weight, down_weight, final_weight)
 
 
 def attend(projected):
@@ -35,7 +372,7 @@
     return head_out.reshape(token_count, local_width).astype(jnp.bfloat16)
 
 
-def local(
+def split(
     tokens,
     conditions,
     ada_block,
@@ -81,6 +418,18 @@
 
 
 def solution(mesh):
+    n = mesh.shape["tp"]
+
+    def local(tokens, cond, ada_block, ada_final, qkv_weight, out_weight, up_weight, down_weight, final_weight):
+        args = (tokens, cond, ada_block, ada_final, qkv_weight, out_weight, up_weight, down_weight, final_weight)
+        gathered = 2 * n * (out_weight.size + up_weight.size + down_weight.size)
+        needed = gathered + 8 * tokens.size + 16 * tokens.shape[0] * HEAD_SIZE
+        one_head = qkv_weight.shape[2] == HEAD_SIZE
+        fits = needed < 24 * 1024 * 1024 and tokens.shape[0] % (64 * n) == 0
+        if n == 8 and mesh.shape["cfg"] == 2 and one_head and fits:
+            return fused(n, *args)
+        return split(*args)
+
     placed = (
         P("dp", None),
         P(("dp", "cfg"), None),

time: 320 us -> 78.4 us (0.25)
  waiting for transfers between devices: 204 us -> 0 us
  Pallas kernels: 0 us -> 72.3 us
  blocking collectives: 51.3 us -> 0 us
  matrix products: 27.3 us -> 0 us
  other arithmetic: 23.7 us -> 0 us
  between operations: 13.3 us -> 0.01 us
  local copies, waits for them, and re-layouts: 0.05 us -> 5.77 us
    psum x3 -> x0, waiting for transfers between devices: 204 us -> none  [the longest x1 103 us: local(): lax.psum(jnp.dot(head_out, out_weight, preferred_element_type=jnp.float32...]
    pallas_call x0 -> x1, Pallas kernels: none -> 72.3 us  [fused(): pl.pallas_call(functools.partial(block_kernel, n), out_shape=jax.ShapeDty...]
    all_gather x2 -> x0, blocking collectives: 51.3 us -> none  [the longest x1 32.3 us: local(): lax.all_gather(block_local, 'tp', axis=0, tiled=True)]
    dot_general x6 -> x0, matrix products: 26.2 us -> none  [the longest x1 8.92 us: local(): jnp.dot(head_out, out_weight, preferred_element_type=jnp.float32)]
    reduce_sum x7 -> x0, other arithmetic: 21.8 us -> none  [the longest x1 8.58 us: attend(): softmaxed = jax.nn.softmax(scores, axis=-1)]
    unnamed x22 -> x2, local copies, waits for them, and re-layouts: 0.05 us -> 3.44 us
  transfers between devices with their start and end apart: 3 -> 0, of which waited for: 3 -> 0; matrix products, arithmetic and copies ran while one was open for 0% -> 0% of each run, Pallas kernels for 0% -> 0%
where the time goes in v1:
time: 78.4 us; the launch traced here: 78.1 us
  Pallas kernels  72.3 us (92%)
  local copies, waits for them, and re-layouts  5.77 us (7%)
    pallas_call x1, Pallas kernels, fused(): pl.pallas_call(functools.partial(block_kernel, n), out_shape=jax.ShapeDty...  72.3 us
    unnamed x2, local copies, waits for them, and re-layouts  3.44 us
    pallas_call x1, local copies, waits for them, and re-layouts, fused(): pl.pallas_call(functools.partial(block_kernel, n), out_shape=jax.ShapeDty...  2.34 us

profile of v1, /device:TPU:0, one launch (start us, length us, event | category | flops | bytes accessed | tf_op | source)
XLA Modules:
  0.0 78.1 jit_solution(15906694138580778629)
XLA Ops:
  0.0 1.6 %copy.11.final_w = bf16[512,64]{1,0:T(8,128)(2,1)} copy(bf16[512,64]{0,1:T(8,128)(2,1)} %param.17) | data formatting | bytes 131072 | tf_op args[8]
  1.6 1.8 %copy.10 = bf16[512,3,64]{2,0,1:T(8,128)(2,1)} copy(bf16[512,3,64]{0,2,1:T(8,128)(2,1)} %param.13) | data formatting | bytes 393216 | tf_op args[4]
  3.4 72.3 %shard_map.91 = f32[2048,64]{1,0:T(8,128)} custom-call(bf16[2048,512]{1,0:T(8,128)(2,1)} %tokens.1, f32[1,256]{1,0:T(1,128)} %cond.1, bf16[256,384]{1,0:T(8,128)(2,1)} %ada_block.1, bf16[256,128]{1,0:T(8,128)(2,1)} %ada_final.1, bf16[3,512,64]{2,1,0:T(8,128)(2,1)} %bitcast.1, bf16[64,512]{1,0:T(8,128)(2,1)} %out_w.1, bf16[512,256]{1,0:T(8,128)(2,1)} %up_w.1, ...), custom_call_target="tpu_custom_call" | custom-call | tf_op jit(solution)/shard_map/pallas_call | solution.py:328
  75.8 2.3 %copy.12 = f32[2048,64]{0,1:T(8,128)} copy(f32[2048,64]{1,0:T(8,128)} %shard_map.91) | data formatting | bytes 1048576 | tf_op jit(solution)/shard_map/pallas_call | solution.py:328

commit v2 on v1

--- a/solution.py
+++ b/solution.py
@@ -12,6 +12,16 @@
 MESH = pl.DeviceIdType.MESH
 F32, BF16 = jnp.float32, jnp.bfloat16
 
+PLAN = {
+    0: ((0, 1), (1, 1)),
+    1: ((2, 1),),
+    2: ((0, 2), (1, 2)),
+    4: ((2, 2), (0, 3)),
+    5: ((1, 3),),
+    6: ((2, 3), (0, 4)),
+}
+LATE = ((1, 4), (2, 4))
+
 guidance = 4.0
 epsilon = 1e-06
 
@@ -51,7 +61,7 @@
     result,
     mod_mine, mod_all, xhat, q_s, k_s, v_s, ho_mine, ho_all, f_out, f_up, f_down,
     half_out, half_in, fin_buf,
-    mod_send, mod_recv, ho_send, ho_recv, g_send, g_recv, h_sem, p_send, p_recv, d_send, d_recv,
+    mod_send, mod_recv, ho_send, ho_recv, z_send, z_recv, x_send, x_recv, y_send, y_recv, s_send, s_recv, h_sem, p_send, p_recv, d_send, d_recv,
 ):
     me = lax.axis_index("tp")
     c = lax.axis_index("cfg")
@@ -61,8 +71,9 @@
     nz = n // 2
     x, z = lax.rem(me, 2), me // 2
 
-    def at(col, dz):
-        return lax.rem(z + dz + nz, nz) * 2 + lax.rem(x + col, 2)
+    y = lax.axis_index("dp")
+    beside = {"dp": 1 - y}
+    across = {"tp": z * 2 + 1 - x}
 
     barrier = pltpu.get_barrier_semaphore()
     for d in range(1, n):
@@ -70,13 +81,14 @@
             barrier, inc=1, device_id={"tp": lax.rem(me + d, n)}, device_id_type=MESH
         )
     pl.semaphore_signal(barrier, inc=1, device_id=other, device_id_type=MESH)
+    pl.semaphore_signal(barrier, inc=1, device_id=beside, device_id_type=MESH)
 
     raw = cond[...]
     signal = jnp.broadcast_to(raw / (1.0 + jnp.exp(-raw)), (8, raw.shape[1])).astype(BF16)
     nb, nf = ada_block.shape[1], ada_final.shape[1]
     mod_mine[0, :, :nb] = dot(signal, ada_block[...])[0:1]
     mod_mine[0, :, nb:] = dot(signal, ada_final[...])[0:1]
-    pl.semaphore_wait(barrier, n)
+    pl.semaphore_wait(barrier, n + 1)
 
     def mod_copy(d):
         return remote(
@@ -89,65 +101,98 @@
 
     own = (out_w, up_w, down_w)
     full = (f_out, f_up, f_down)
-    places = [
-        (at(1, 0), 0), (at(0, -1), 0), (at(0, 1), 0), (at(1, -1), 0), (at(1, 1), 0),
-        (at(0, 2), 1), (at(0, 2), 2), (at(1, 2), 1), (at(1, 2), 2),
-    ]
-
-    def region(ref, part, core):
-        rows = ref.shape[0]
-        if part == 0:
-            return rows_of(ref, core * (rows // 2), rows // 2)
-        return rows_of(ref, core * (rows // 2) + (part - 1) * (rows // 4), rows // 4)
-
-    plus, minus, across = {"tp": at(0, 1)}, {"tp": at(0, -1)}, {"tp": at(1, 0)}
-    sends = [
-        (me, 0, across), (me, 0, plus), (me, 0, minus),
-        (at(1, 0), 0, plus), (at(1, 0), 0, minus),
-        (at(0, -1), 1, plus), (at(0, 1), 2, minus),
-        (at(1, -1), 1, plus), (at(1, 1), 2, minus),
-    ]
-    links = len(sends)
-
-    def link(k, j):
-        owner, part, where = sends[j]
-        src = own[k] if j < 3 else full[k].at[owner]
+    h = HEAD_SIZE
+
+    def region(ref, k, core, plane=None):
+        base, rows = 0, own[k].shape[0]
+        if k == 0 and ref is not out_w:
+            base = h
+        size = rows // 2
+        start = base + core * size
+        if plane is not None:
+            size = size // 2
+            start = start + plane * size
+        return rows_of(ref, start, size)
+
+    def fetched(k, owner):
+        return region(full[k].at[owner], k, c, y if k == 2 else None)
+
+    def z_copy(k, zo, way, mine=False):
+        owner = zo * 2 + x
+        src = region(own[k], k, c, y if k == 2 else None) if mine else fetched(k, owner)
         return remote(
-            region(src, part, c), region(full[k].at[owner], part, c),
-            g_send.at[k, j], g_recv.at[k, j], where,
+            src, fetched(k, owner), z_send.at[k, zo, way], z_recv.at[k, zo],
+            {"tp": (z + 1 - 2 * way) * 2 + x},
         )
 
-    def landed(k, j):
-        owner, part = places[j]
-        dst = region(full[k].at[owner], part, c)
-        return remote(dst, dst, g_send.at[k, j], g_recv.at[k, j], across)
-
-    def share(k, j):
-        owner, part = places[j]
-        dst = region(full[k].at[owner], part, c)
-        return remote(dst, dst, g_send.at[k, links + j], g_recv.at[k, links + j], other)
-
-    def shared(k, j):
-        owner, part = places[j]
-        dst = region(full[k].at[owner], part, 1 - c)
-        return remote(dst, dst, g_send.at[k, links + j], g_recv.at[k, links + j], other)
-
-    def open_gather(k):
-        for j in (0, 1, 2):
-            link(k, j).start()
-
-    def forward(k, arrivals, starts):
-        for j in arrivals:
-            landed(k, j).wait_recv()
-        for j in starts:
-            link(k, j).start()
-        for j in arrivals:
-            share(k, j).start()
-
-    open_gather(0)
-    open_gather(1)
+    def x_copy(k, zo, mine=False):
+        owner = zo * 2 + x
+        src = region(own[k], k, c, y if k == 2 else None) if mine else fetched(k, owner)
+        return remote(src, fetched(k, owner), x_send.at[k, zo], x_recv.at[k, zo], across)
+
+    def y_copy(owner, plane):
+        dst = region(f_down.at[owner], 2, c, plane)
+        return remote(dst, dst, y_send.at[owner], y_recv.at[owner], beside)
+
+    def core_copy(k, owner, core):
+        dst = region(full[k].at[owner], k, core)
+        return remote(dst, dst, s_send.at[k, owner], s_recv.at[k, owner], other)
+
+    def hand_on(k, owner):
+        if k == 2:
+            y_copy(owner, y).start()
+        else:
+            core_copy(k, owner, c).start()
+
+    def stage(k, dist):
+        if dist == 0:
+            for way in (0, 1):
+                @pl.when(z < nz - 1 if way == 0 else z > 0)
+                def _():
+                    z_copy(k, z, way, True).start()
+            x_copy(k, z, True).start()
+            return
+        for way in (0, 1):
+            zo = z - dist if way == 0 else z + dist
+            inside = zo >= 0 if way == 0 else zo < nz
+
+            if dist < nz:
+                @pl.when(inside)
+                def _():
+                    z_copy(k, zo, way).wait_recv()
+                    @pl.when(z < nz - 1 if way == 0 else z > 0)
+                    def _():
+                        z_copy(k, zo, way).start()
+                    x_copy(k, zo).start()
+                    hand_on(k, zo * 2 + x)
+
+            zx = z - dist + 1 if way == 0 else z + dist - 1
+            if dist > 1 or way == 0:
+                @pl.when(zx >= 0 if way == 0 else zx < nz)
+                def _():
+                    place = fetched(k, zx * 2 + 1 - x)
+                    remote(place, place, x_send.at[k, zx], x_recv.at[k, zx], across).wait_recv()
+                    hand_on(k, zx * 2 + 1 - x)
+
+    def share_down():
+        for d in range(1, n):
+            owner = lax.rem(me + d, n)
+            y_copy(owner, 1 - y).wait_recv()
+            core_copy(2, owner, c).start()
+
+    def arrived(k):
+        for d in range(1, n):
+            core_copy(k, lax.rem(me + d, n), 1 - c).wait_recv()
+
     for k in range(3):
-        full[k][me] = own[k][...]
+        stage(k, 0)
+    empty = jnp.zeros((h, width), BF16)
+    for t in range(n):
+        f_out[t, :h] = empty
+        f_out[t, 2 * h :] = empty
+    f_out[me, h : 2 * h] = out_w[...]
+    f_up[me] = up_w[...]
+    f_down[me] = down_w[...]
 
     def norm_step(i, _):
         r = pl.ds(pl.multiple_of(i * shard, shard), shard)
@@ -172,16 +217,19 @@
     shift1, scale1, gate1, shift2, scale2, gate2 = [mod_row(0, nb, r) for r in range(6)]
     shift_f, scale_f = [mod_row(nb, nf, r) for r in range(2)]
 
-    h = HEAD_SIZE
-    ones = (lax.broadcasted_iota(jnp.int32, (shard, h), 1) == 0).astype(F32).astype(BF16)
+    lanes = lax.broadcasted_iota(jnp.int32, (shard, 2 * h), 1)
+    upper = (lanes >= h).astype(F32)
+    v_w, none = qkv[2], jnp.zeros((h, width), BF16)
+    v_low = jnp.concatenate([v_w, none], axis=0)
+    v_high = jnp.concatenate([none, v_w], axis=0)
 
     def qkv_step(i, _):
         r = pl.ds(pl.multiple_of(i * shard, shard), shard)
         normed = (xhat[r, :] * (1.0 + scale1) + shift1).astype(BF16)
-        q_s[r, :] = (dot(normed, qkv[0]) * (h ** -0.5 * math.log2(math.e))).astype(BF16)
-        k_s[r, :] = dot(normed, qkv[1]).astype(BF16)
-        v_s[r, :h] = dot(normed, qkv[2]).astype(BF16)
-        v_s[r, h:] = ones
+        q_s[r, :] = (dot_nt(normed, qkv[0]) * (h ** -0.5 * math.log2(math.e))).astype(BF16)
+        k_s[r, :] = dot_nt(normed, qkv[1]).astype(BF16)
+        v_s[0, r, :] = (dot_nt(normed, v_low) + upper).astype(BF16)
+        v_s[1, r, :] = (dot_nt(normed, v_high) + (1.0 - upper)).astype(BF16)
         return 0
 
     lax.fori_loop(0, count // shard, qkv_step, 0)
@@ -195,39 +243,23 @@
     sub = shard // 2
 
     def attend_step(i, _):
-        @pl.when(i == 0)
-        def _():
-            for k in (0, 1):
-                forward(k, (0, 1, 2), (3, 4, 5, 6))
-            open_gather(2)
-
-        @pl.when(i == 3)
-        def _():
-            for k in (0, 1):
-                forward(k, (3, 4), (7, 8))
-
-        @pl.when(i == 4)
-        def _():
-            forward(2, (0, 1, 2), (3, 4, 5, 6))
-            for k in (0, 1):
-                forward(k, (5, 6), ())
-
-        @pl.when(i == 6)
-        def _():
-            forward(2, (3, 4), (7, 8))
-            for k in (0, 1):
-                forward(k, (7, 8), ())
+        for when, steps in PLAN.items():
+            @pl.when(i == when)
+            def _():
+                for k, dist in steps:
+                    stage(k, dist)
 
         peer = lax.rem(me + 1 + i, n)
-        for part in range(shard // sub):
+        parts = []
+        for part in range(2):
             r = pl.ds(pl.multiple_of(peer * shard + part * sub, sub), sub)
             scores = dot_nt(q_s[r, :], k_s[...])
             top = jnp.max(scores, axis=-1, keepdims=True)
             weights = jnp.exp2(scores - top).astype(BF16)
-            mixed = dot(weights, v_s[...])
-            ho_mine[i, part * sub : (part + 1) * sub, :] = (
-                mixed[:, :h] / mixed[:, h : h + 1]
-            ).astype(BF16)
+            mixed = dot(weights, v_s[part])
+            total = mixed[:, h : h + 1] if part == 0 else mixed[:, 0:1]
+            parts.append(mixed / total)
+        ho_mine[i] = jnp.where(lanes[:sub] < h, parts[0], parts[1]).astype(BF16)
 
         @pl.when(i < n - 1)
         def _():
@@ -236,28 +268,30 @@
         return 0
 
     lax.fori_loop(0, n, attend_step, 0)
-    forward(2, (5, 6), ())
+    for k, dist in LATE:
+        stage(k, dist)
 
     ho_all[me] = ho_mine[n - 1]
-    for j in range(links):
-        shared(0, j).wait_recv()
+    arrived(0)
     for i in range(n - 1):
         origin = ho_all.at[lax.rem(me - 1 - i + n, n)]
         remote(origin, origin, ho_send.at[i], ho_recv.at[i], across).wait_recv()
-    attended = dot(ho_all[0], f_out[0])
-    for t in range(1, n):
-        attended += dot(ho_all[t], f_out[t])
+    def project(lo):
+        sums = dot(ho_all[0], f_out[0, lo : lo + 2 * h])
+        for t in range(1, n):
+            sums += dot(ho_all[t], f_out[t, lo : lo + 2 * h])
+        return sums
+
+    attended = jnp.concatenate([project(h), project(0)], axis=0)
     r = pl.ds(pl.multiple_of(me * shard, shard), shard)
     stream = tokens[r, :].astype(F32) + gate1 * attended
     normed = modulate(stream, scale2, shift2)
-    forward(2, (7, 8), ())
-    for j in range(links):
-        shared(1, j).wait_recv()
+    share_down()
+    arrived(1)
     hidden = [
         jax.nn.gelu(dot(normed, f_up[t]), approximate=True).astype(BF16) for t in range(n)
     ]
-    for j in range(links):
-        shared(2, j).wait_recv()
+    arrived(2)
     mlp = dot(hidden[0], f_down[0])
     for t in range(1, n):
         mlp += dot(hidden[t], f_down[t])
@@ -265,14 +299,10 @@
     final_in = modulate(stream, scale_f, shift_f)
 
     weighting = jnp.where(c == 0, guidance, 1.0 - guidance).astype(F32)
-    out_width = final_w.shape[1]
-    predicted = weighting * dot(final_in, final_w[...])
-    quarter = shard // 4
+    predicted = weighting * dot_nt(final_w[...], final_in)
+    part = shard // 2
     for half in range(2):
-        lo = half * 2 * quarter
-        half_out[half, :, :] = jnp.concatenate(
-            [predicted[lo : lo + quarter], predicted[lo + quarter : lo + 2 * quarter]], axis=1
-        )
+        half_out[half] = predicted[:, half * part : (half + 1) * part]
     trade = remote(half_out.at[1 - c], half_in, h_sem.at[0], h_sem.at[1], other)
     trade.start()
     trade.wait()
@@ -300,10 +330,8 @@
         hand(d, 1 - c).wait_recv()
     for t in range(n):
         for half in range(2):
-            both = fin_buf[t, half].astype(F32)
-            lo = t * shard + half * 2 * quarter
-            result[lo : lo + quarter, :] = both[:, :out_width]
-            result[lo + quarter : lo + 2 * quarter, :] = both[:, out_width:]
+            lo = t * shard + half * part
+            result[:, lo : lo + part] = fin_buf[t, half]
 
     for d in range(1, n):
         mod_copy(d).wait_send()
@@ -312,22 +340,33 @@
     for d in range(n):
         hand(d, c).wait_send()
     for k in range(3):
-        for j in range(links):
-            link(k, j).wait_send()
-            share(k, j).wait_send()
+        for zo in range(nz):
+            x_copy(k, zo).wait_send()
+        for way in (0, 1):
+            @pl.when(z < nz - 1 if way == 0 else z > 0)
+            def _():
+                for dist in range(nz):
+                    zo = z - dist if way == 0 else z + dist
+                    @pl.when(zo >= 0 if way == 0 else zo < nz)
+                    def _():
+                        z_copy(k, zo, way).wait_send()
+        for d in range(1, n):
+            core_copy(k, lax.rem(me + d, n), c).wait_send()
+    for d in range(1, n):
+        y_copy(lax.rem(me + d, n), y).wait_send()
 
 
 def fused(n, tokens, cond, ada_block, ada_final, qkv_weight, out_weight, up_weight, down_weight, final_weight):
     count, width = tokens.shape
     shard = count // n
-    qkv = jnp.transpose(qkv_weight, (1, 0, 2))
+    qkv = jnp.transpose(qkv_weight, (1, 2, 0))
     mod = ada_block.shape[1] + ada_final.shape[1]
     h, out_width = HEAD_SIZE, final_weight.shape[1]
     dma = pltpu.SemaphoreType.DMA
     vm = pl.BlockSpec(memory_space=pltpu.VMEM)
-    return pl.pallas_call(
+    guided = pl.pallas_call(
         functools.partial(block_kernel, n),
-        out_shape=jax.ShapeDtypeStruct((count, out_width), F32),
+        out_shape=jax.ShapeDtypeStruct((out_width, count), BF16),
         in_specs=[vm] * 9,
         out_specs=vm,
         scratch_shapes=[
@@ -336,18 +375,21 @@
             pltpu.VMEM((count, width), F32),
             pltpu.VMEM((count, h), BF16),
             pltpu.VMEM((count, h), BF16),
-            pltpu.VMEM((count, 2 * h), BF16),
-            pltpu.VMEM((n, shard, h), BF16),
-            pltpu.VMEM((n, shard, h), BF16),
-            pltpu.VMEM((n,) + out_weight.shape, BF16),
+            pltpu.VMEM((2, count, 2 * h), BF16),
+            pltpu.VMEM((n, shard // 2, 2 * h), BF16),
+            pltpu.VMEM((n, shard // 2, 2 * h), BF16),
+            pltpu.VMEM((n, 3 * h, width), BF16),
             pltpu.VMEM((n,) + up_weight.shape, BF16),
             pltpu.VMEM((n,) + down_weight.shape, BF16),
-            pltpu.VMEM((2, shard // 4, 2 * out_width), F32),
-            pltpu.VMEM((shard // 4, 2 * out_width), F32),
-            pltpu.VMEM((n, 2, shard // 4, 2 * out_width), BF16),
+            pltpu.VMEM((2, out_width, shard // 2), F32),
+            pltpu.VMEM((out_width, shard // 2), F32),
+            pltpu.VMEM((n, 2, out_width, shard // 2), BF16),
             dma((n - 1,)), dma((n - 1,)),
             dma((n - 1,)), dma((n - 1,)),
-            dma((3, 18)), dma((3, 18)),
+            dma((3, n // 2, 2)), dma((3, n // 2)),
+            dma((3, n // 2)), dma((3, n // 2)),
+            dma((n,)), dma((n,)),
+            dma((3, n)), dma((3, n)),
             dma((2,)),
             dma((n,)), dma((n,)),
             dma((n,)), dma((n,)),
@@ -355,7 +397,8 @@
         compiler_params=pltpu.CompilerParams(
             collective_id=0, has_side_effects=True, vmem_limit_bytes=60 * 1024 * 1024
         ),
-    )(tokens, cond, ada_block, ada_final, qkv, out_weight, up_weight, down_weight, final_weight)
+    )(tokens, cond, ada_block, ada_final, qkv, out_weight, up_weight, down_weight, final_weight.T)
+    return guided.astype(F32).T
 
 
 def attend(projected):
@@ -425,8 +468,9 @@
         gathered = 2 * n * (out_weight.size + up_weight.size + down_weight.size)
         needed = gathered + 8 * tokens.size + 16 * tokens.shape[0] * HEAD_SIZE
         one_head = qkv_weight.shape[2] == HEAD_SIZE
-        fits = needed < 24 * 1024 * 1024 and tokens.shape[0] % (64 * n) == 0
-        if n == 8 and mesh.shape["cfg"] == 2 and one_head and fits:
+        fits = needed < 24 * 1024 * 1024 and tokens.shape[0] % (256 * n) == 0
+        pairs = mesh.shape["cfg"] == 2 and mesh.shape["dp"] == 2
+        if n == 8 and pairs and one_head and fits:
             return fused(n, *args)
         return split(*args)
 

time: 78.4 us -> 54.3 us (0.69)
  Pallas kernels: 72.3 us -> 52.3 us
  local copies, waits for them, and re-layouts: 5.77 us -> 0 us
  other arithmetic: 0 us -> 1.78 us
    pallas_call x1, Pallas kernels: 72.3 us -> 52.3 us  [fused(): pl.pallas_call(functools.partial(block_kernel, n), out_shape=jax.ShapeDty...]
    unnamed x2 -> x0, local copies, waits for them, and re-layouts: 3.44 us -> none
    pallas_call x1 -> x0, local copies, waits for them, and re-layouts: 2.34 us -> none  [fused(): pl.pallas_call(functools.partial(block_kernel, n), out_shape=jax.ShapeDty...]
    transpose x0 -> x1, other arithmetic: none -> 1.78 us  [fused(): return guided.astype(F32).T]
where the time goes in v2:
time: 54.3 us; the launch traced here: 54.1 us
  Pallas kernels  52.3 us (96%)
  other arithmetic  1.78 us (3%)
    pallas_call x1, Pallas kernels, fused(): pl.pallas_call(functools.partial(block_kernel, n), out_shape=jax.ShapeDty...  52.3 us
    transpose x1, other arithmetic, fused(): return guided.astype(F32).T  1.78 us

profile of v2, /device:TPU:0, one launch (start us, length us, event | category | flops | bytes accessed | tf_op | source)
XLA Modules:
  0.0 54.1 jit_solution(661111950717799123)
XLA Ops:
  0.0 52.3 %shard_map.91 = bf16[64,2048]{1,0:T(8,128)(2,1)} custom-call(bf16[2048,512]{1,0:T(8,128)(2,1)} %tokens.1, f32[1,256]{1,0:T(1,128)} %cond.1, bf16[256,384]{1,0:T(8,128)(2,1)} %ada_block.1, bf16[256,128]{1,0:T(8,128)(2,1)} %ada_final.1, bf16[3,64,512]{2,1,0:T(8,128)(2,1)} %bitcast.4, bf16[64,512]{1,0:T(8,128)(2,1)} %out_w.1, bf16[512,256]{1,0:T(8,128)(2,1)} %up_w.1, ...), custom_call_target="tpu_custom_call" | custom-call | tf_op jit(solution)/shard_map/pallas_call | solution.py:367
  52.3 1.8 %convert_bitcast_fusion = f32[2048,64]{0,1:T(8,128)} fusion(bf16[64,2048]{1,0:T(8,128)(2,1)} %shard_map.91), kind=kLoop, calls=%fused_computation | loop fusion | flops 131072 | bytes 786432 | tf_op jit(solution)/shard_map/transpose | solution.py:401

commit v3 on v2

--- a/solution.py
+++ b/solution.py
@@ -12,15 +12,15 @@
 MESH = pl.DeviceIdType.MESH
 F32, BF16 = jnp.float32, jnp.bfloat16
 
+SHARE = 10
+EARLY = ((0, 1), (1, 1))
+QKV_PLAN = {4: ((2, 1), (3, 1)), 7: ((0, 2), (1, 2))}
 PLAN = {
-    0: ((0, 1), (1, 1)),
-    1: ((2, 1),),
-    2: ((0, 2), (1, 2)),
-    4: ((2, 2), (0, 3)),
-    5: ((1, 3),),
-    6: ((2, 3), (0, 4)),
+    1: ((2, 2), (3, 2)), 2: ((0, 3), (2, 11), (3, 11)), 3: ((1, 3),), 4: ((2, 3), (3, 3)),
+    5: ((0, 4), (2, 12), (3, 12)), 6: ((1, 4),), 7: ((2, 4), (2, 13)),
 }
-LATE = ((1, 4), (2, 4))
+LATE = ((3, 4), (3, 13), (2, 14))
+LAST = ((3, 14),)
 
 guidance = 4.0
 epsilon = 1e-06
@@ -99,12 +99,17 @@
     for d in range(1, n):
         mod_copy(d).start()
 
-    own = (out_w, up_w, down_w)
-    full = (f_out, f_up, f_down)
+    half_up = up_w.shape[0] // 2
+    own = (out_w, up_w, up_w, down_w)
+    full = (f_out, f_up, f_up, f_down)
+    first = (0, 0, half_up, 0)
+    extent = (out_w.shape[0], half_up, half_up, down_w.shape[0])
+    paired = (False, False, True, True)
+    kinds = len(own)
     h = HEAD_SIZE
 
     def region(ref, k, core, plane=None):
-        base, rows = 0, own[k].shape[0]
+        base, rows = first[k], extent[k]
         if k == 0 and ref is not out_w:
             base = h
         size = rows // 2
@@ -115,11 +120,11 @@
         return rows_of(ref, start, size)
 
     def fetched(k, owner):
-        return region(full[k].at[owner], k, c, y if k == 2 else None)
+        return region(full[k].at[owner], k, c, y if paired[k] else None)
 
     def z_copy(k, zo, way, mine=False):
         owner = zo * 2 + x
-        src = region(own[k], k, c, y if k == 2 else None) if mine else fetched(k, owner)
+        src = region(own[k], k, c, y if paired[k] else None) if mine else fetched(k, owner)
         return remote(
             src, fetched(k, owner), z_send.at[k, zo, way], z_recv.at[k, zo],
             {"tp": (z + 1 - 2 * way) * 2 + x},
@@ -127,24 +132,27 @@
 
     def x_copy(k, zo, mine=False):
         owner = zo * 2 + x
-        src = region(own[k], k, c, y if k == 2 else None) if mine else fetched(k, owner)
+        src = region(own[k], k, c, y if paired[k] else None) if mine else fetched(k, owner)
         return remote(src, fetched(k, owner), x_send.at[k, zo], x_recv.at[k, zo], across)
 
-    def y_copy(owner, plane):
-        dst = region(f_down.at[owner], 2, c, plane)
-        return remote(dst, dst, y_send.at[owner], y_recv.at[owner], beside)
+    def y_copy(k, owner, plane):
+        dst = region(full[k].at[owner], k, c, plane)
+        return remote(dst, dst, y_send.at[k, owner], y_recv.at[k, owner], beside)
 
     def core_copy(k, owner, core):
         dst = region(full[k].at[owner], k, core)
         return remote(dst, dst, s_send.at[k, owner], s_recv.at[k, owner], other)
 
     def hand_on(k, owner):
-        if k == 2:
-            y_copy(owner, y).start()
+        if paired[k]:
+            y_copy(k, owner, y).start()
         else:
             core_copy(k, owner, c).start()
 
     def stage(k, dist):
+        if dist > SHARE:
+            share(k, dist - SHARE)
+            return
         if dist == 0:
             for way in (0, 1):
                 @pl.when(z < nz - 1 if way == 0 else z > 0)
@@ -174,17 +182,35 @@
                     remote(place, place, x_send.at[k, zx], x_recv.at[k, zx], across).wait_recv()
                     hand_on(k, zx * 2 + 1 - x)
 
-    def share_down():
-        for d in range(1, n):
-            owner = lax.rem(me + d, n)
-            y_copy(owner, 1 - y).wait_recv()
-            core_copy(2, owner, c).start()
+    def steps_at(plan, i):
+        for when, steps in plan.items():
+            @pl.when(i == when)
+            def _():
+                for k, dist in steps:
+                    stage(k, dist)
+
+    def share(k, dist):
+        def one(owner):
+            y_copy(k, owner, 1 - y).wait_recv()
+            core_copy(k, owner, c).start()
+
+        for way in (0, 1):
+            zo = z - dist if way == 0 else z + dist
+            if dist < nz:
+                @pl.when(zo >= 0 if way == 0 else zo < nz)
+                def _():
+                    one(zo * 2 + x)
+            zx = z - dist + 1 if way == 0 else z + dist - 1
+            if dist > 1 or way == 0:
+                @pl.when(zx >= 0 if way == 0 else zx < nz)
+                def _():
+                    one(zx * 2 + 1 - x)
 
     def arrived(k):
         for d in range(1, n):
             core_copy(k, lax.rem(me + d, n), 1 - c).wait_recv()
 
-    for k in range(3):
+    for k in range(kinds):
         stage(k, 0)
     empty = jnp.zeros((h, width), BF16)
     for t in range(n):
@@ -223,7 +249,11 @@
     v_low = jnp.concatenate([v_w, none], axis=0)
     v_high = jnp.concatenate([none, v_w], axis=0)
 
+    for k, dist in EARLY:
+        stage(k, dist)
+
     def qkv_step(i, _):
+        steps_at(QKV_PLAN, i)
         r = pl.ds(pl.multiple_of(i * shard, shard), shard)
         normed = (xhat[r, :] * (1.0 + scale1) + shift1).astype(BF16)
         q_s[r, :] = (dot_nt(normed, qkv[0]) * (h ** -0.5 * math.log2(math.e))).astype(BF16)
@@ -243,11 +273,7 @@
     sub = shard // 2
 
     def attend_step(i, _):
-        for when, steps in PLAN.items():
-            @pl.when(i == when)
-            def _():
-                for k, dist in steps:
-                    stage(k, dist)
+        steps_at(PLAN, i)
 
         peer = lax.rem(me + 1 + i, n)
         parts = []
@@ -286,12 +312,14 @@
     r = pl.ds(pl.multiple_of(me * shard, shard), shard)
     stream = tokens[r, :].astype(F32) + gate1 * attended
     normed = modulate(stream, scale2, shift2)
-    share_down()
     arrived(1)
+    arrived(2)
     hidden = [
         jax.nn.gelu(dot(normed, f_up[t]), approximate=True).astype(BF16) for t in range(n)
     ]
-    arrived(2)
+    for k, dist in LAST:
+        stage(k, dist)
+    arrived(3)
     mlp = dot(hidden[0], f_down[0])
     for t in range(1, n):
         mlp += dot(hidden[t], f_down[t])
@@ -339,7 +367,7 @@
         ho_copy(d - 1).wait_send()
     for d in range(n):
         hand(d, c).wait_send()
-    for k in range(3):
+    for k in range(kinds):
         for zo in range(nz):
             x_copy(k, zo).wait_send()
         for way in (0, 1):
@@ -352,8 +380,9 @@
                         z_copy(k, zo, way).wait_send()
         for d in range(1, n):
             core_copy(k, lax.rem(me + d, n), c).wait_send()
-    for d in range(1, n):
-        y_copy(lax.rem(me + d, n), y).wait_send()
+        for d in range(1, n):
+            if paired[k]:
+                y_copy(k, lax.rem(me + d, n), y).wait_send()
 
 
 def fused(n, tokens, cond, ada_block, ada_final, qkv_weight, out_weight, up_weight, down_weight, final_weight):
@@ -386,10 +415,10 @@
             pltpu.VMEM((n, 2, out_width, shard // 2), BF16),
             dma((n - 1,)), dma((n - 1,)),
             dma((n - 1,)), dma((n - 1,)),
-            dma((3, n // 2, 2)), dma((3, n // 2)),
-            dma((3, n // 2)), dma((3, n // 2)),
-            dma((n,)), dma((n,)),
-            dma((3, n)), dma((3, n)),
+            dma((4, n // 2, 2)), dma((4, n // 2)),
+            dma((4, n // 2)), dma((4, n // 2)),
+            dma((4, n)), dma((4, n)),
+            dma((4, n)), dma((4, n)),
             dma((2,)),
             dma((n,)), dma((n,)),
             dma((n,)), dma((n,)),

time: 54.3 us -> 49.2 us (0.906)
  Pallas kernels: 52.3 us -> 47.3 us
    pallas_call x1, Pallas kernels: 52.3 us -> 47.3 us  [fused(): pl.pallas_call(functools.partial(block_kernel, n), out_shape=jax.ShapeDty...]
where the time goes in v3:
time: 49.2 us; the launch traced here: 49.1 us
  Pallas kernels  47.3 us (96%)
  other arithmetic  1.78 us (4%)
    pallas_call x1, Pallas kernels, fused(): pl.pallas_call(functools.partial(block_kernel, n), out_shape=jax.ShapeDty...  47.3 us
    transpose x1, other arithmetic, fused(): return guided.astype(F32).T  1.78 us

profile of v3, /device:TPU:0, one launch (start us, length us, event | category | flops | bytes accessed | tf_op | source)
XLA Modules:
  0.0 49.1 jit_solution(17496785215000308689)
XLA Ops:
  0.0 47.3 %shard_map.91 = bf16[64,2048]{1,0:T(8,128)(2,1)} custom-call(bf16[2048,512]{1,0:T(8,128)(2,1)} %tokens.1, f32[1,256]{1,0:T(1,128)} %cond.1, bf16[256,384]{1,0:T(8,128)(2,1)} %ada_block.1, bf16[256,128]{1,0:T(8,128)(2,1)} %ada_final.1, bf16[3,64,512]{2,1,0:T(8,128)(2,1)} %bitcast.4, bf16[64,512]{1,0:T(8,128)(2,1)} %out_w.1, bf16[512,256]{1,0:T(8,128)(2,1)} %up_w.1, ...), custom_call_target="tpu_custom_call" | custom-call | tf_op jit(solution)/shard_map/pallas_call | solution.py:396
  47.3 1.8 %convert_bitcast_fusion = f32[2048,64]{0,1:T(8,128)} fusion(bf16[64,2048]{1,0:T(8,128)(2,1)} %shard_map.91), kind=kLoop, calls=%fused_computation | loop fusion | flops 131072 | bytes 786432 | tf_op jit(solution)/shard_map/transpose | solution.py:430
